TPU v7x, 256 devices: a whole 4x4x8 slice. The times are simulated.
256 devices in a mesh: tm: 64 (over x, z, core), hid: 4 (over y).
Axes of the slice: x: 4, y: 4, z: 8, core: 2. Of those that a mesh axis runs over, the one named last changes fastest.
Arguments:
- token_ids: int32 [32768], P('tm'), may hold values from 0 to 255
- input_table: float32 [256, 3, 2048], P(None, None, 'hid'), may hold values from -6 to 6
- recur_weight: bfloat16 [2048, 3, 2048], P(None, None, 'hid'), may hold values from -0.125 to 0.125
- z_bias: float32 [2048], P('hid'), may hold values from -1 to 9
- hn_bias: float32 [2048], P('hid'), may hold values from -4 to 4
- init_state: float32 [2048], P('hid'), may hold values from -0.9 to 0.9
- guess: float32 [32768, 2048], P('tm', 'hid'), may hold values from -3 to 3
Outputs:
- states: float32 [32768, 2048], P('tm', 'hid')
- residual_norm: float32 [2], replicated
All inputs are finite; a program needn't handle non-finite values.
Results may differ from a plain program's by a relative error of at most 0.00063.
Values may be sent and summed in bfloat16 or wider, within the bound.
A program may use at most 128 MiB of HBM per device.

v0:
```python
import functools

import jax
import jax.numpy as jnp
from jax import lax
from jax.experimental import pallas as pl
from jax.experimental.pallas import tpu as pltpu
from jax.sharding import Mesh
from jax.sharding import PartitionSpec as P

ITERS = 2
SEGS = 8
PAIRS = 4
LANES = 128
ORDER = (1, 0, 2, 3)
TM = ("tm_0", "tm_1", "tm_2")
MESH = pl.DeviceIdType.MESH
F32 = jnp.float32
BF16 = jnp.bfloat16


def dot(a, b):
    return jnp.dot(a, b, preferred_element_type=F32)


def sigmoid(x):
    return 0.5 * jnp.tanh(0.5 * x) + 0.5


def lanes_to_rows(row):
    return jnp.concatenate([row[:, k : k + LANES] for k in range(0, row.shape[1], LANES)], 0)


def rows_to_lanes(block):
    return jnp.concatenate([block[k : k + 1] for k in range(block.shape[0])], 1)


def wait_bytes(ref, sem):
    pltpu.make_async_copy(ref, ref, sem).wait()


def kernel(
    dims,
    ids_ref,
    table_hbm,
    weight_hbm,
    zb_ref,
    hb_ref,
    init_ref,
    guess_hbm,
    out_hbm,
    res_ref,
    table,
    pieces,
    weight,
    hist,
    sent,
    onehot,
    inp,
    acc,
    pre_a,
    pre_b,
    diag,
    seg,
    edge,
    line_maps,
    x_maps,
    line_res,
    plane_res,
    in_sem,
    weight_sem,
    out_sem,
    edge_sem,
    send_sem,
    recv_sem,
    relay_sem,
    line_sem,
    x_sem,
    res_sem,
):
    nx, nz, nc, ny, rows, width, vocab = dims
    steps = rows // SEGS
    block = rows // PAIRS
    group = block // SEGS
    tiles = width // LANES
    members = nz * nc
    plane = nx * ny
    x, z, c, y = (lax.axis_index(a) for a in (*TM, "hid"))
    mine = z * nc + c
    tm = x * members + mine
    right, left, far = (lax.rem(y + d, ny) for d in (1, ny - 1, 2))
    count = nx * members * rows * ny * width

    def line_peer(k):
        peer = lax.rem(mine + k, members)
        return {"tm_1": peer // nc, "tm_2": lax.rem(peer, nc)}

    def plane_peer(k):
        return {"tm_0": lax.rem(x + k // ny, nx), "hid": lax.rem(y + lax.rem(k, ny), ny)}

    def tm_peer(index):
        return {
            "tm_0": index // members,
            "tm_1": lax.rem(index, members) // nc,
            "tm_2": lax.rem(index, nc),
        }

    total = nx * members
    after, before = (lax.rem(tm + d, total) for d in (1, total - 1))

    barrier = pltpu.get_barrier_semaphore()

    def greet(peer):
        pl.semaphore_signal(barrier, inc=1, device_id=peer, device_id_type=MESH)

    greet(tm_peer(after))
    greet(tm_peer(before))
    lax.fori_loop(1, plane, lambda k, _: greet(plane_peer(k)), None)
    lax.fori_loop(1, members, lambda k, _: greet(line_peer(k)), None)

    for s in range(SEGS):
        pltpu.make_async_copy(
            guess_hbm.at[pl.ds(s * steps, steps)], hist.at[pl.ds(1, steps), s], in_sem.at[s]
        ).start()
    for s in range(SEGS):
        pltpu.make_async_copy(
            guess_hbm.at[pl.ds(s * steps, steps)], hist.at[pl.ds(1, steps), s], in_sem.at[s]
        ).wait()
    table_copy = pltpu.make_async_copy(table_hbm, table, weight_sem.at[0])
    weight_copy = pltpu.make_async_copy(weight_hbm, weight, weight_sem.at[1])
    pl.semaphore_wait(barrier, plane + members)

    edge_copy = pltpu.make_async_remote_copy(
        src_ref=hist.at[steps],
        dst_ref=edge,
        send_sem=edge_sem.at[0],
        recv_sem=edge_sem.at[1],
        device_id=tm_peer(after),
        device_id_type=MESH,
    )
    edge_copy.start()

    def piece(it, slot, p):
        return sent.at[it, slot, pl.ds(p * block, block)]

    def half(it, slot, p, h):
        return sent.at[it, slot, pl.ds(p * block + h * (block // 2), block // 2)]

    def direct(it, p, side, slot):
        return pltpu.make_async_remote_copy(
            src_ref=piece(it, slot, p),
            dst_ref=piece(it, slot, p),
            send_sem=send_sem.at[it],
            recv_sem=recv_sem.at[it, side, p],
            device_id={"hid": (right, left)[side]},
            device_id_type=MESH,
        )

    def relay(it, p, side, slot):
        return pltpu.make_async_remote_copy(
            src_ref=half(it, slot, p, side),
            dst_ref=half(it, slot, p, side),
            send_sem=send_sem.at[it],
            recv_sem=relay_sem.at[it, side, p],
            device_id={"hid": (right, left)[side]},
            device_id_type=MESH,
        )

    def block_rows(p):
        return pl.ds(pl.multiple_of(p * block, block), block)

    def weight_rows(slot):
        return pl.ds(pl.multiple_of(slot * width, width), width)

    def send_block(it, p):
        prev = hist[pl.ds(p * group, group)].reshape(block, width)
        sent[it, y, block_rows(p)] = prev.astype(BF16)
        direct(it, p, 0, y).start()
        direct(it, p, 1, y).start()

    def near_products(it):
        def visit(i, _):
            p = jnp.where(i < 2, 1 - i, i)
            direct(it, p, 0, left).wait_recv()
            relay(it, p, 0, left).start()
            direct(it, p, 1, right).wait_recv()
            relay(it, p, 1, right).start()

            def gate(g, _):
                part = dot(sent[it, y, block_rows(p)], weight[g, weight_rows(y)])
                part += dot(sent[it, left, block_rows(p)], weight[g, weight_rows(left)])
                part += dot(sent[it, right, block_rows(p)], weight[g, weight_rows(right)])
                acc[g, block_rows(p)] = part

            lax.fori_loop(0, 3, gate, None)

        lax.fori_loop(0, PAIRS, visit, None)

    def far_products(it, p):
        relay(it, p, 0, far).wait_recv()
        relay(it, p, 1, far).wait_recv()

        def gate(g, _):
            acc[g, block_rows(p)] += dot(sent[it, far, block_rows(p)], weight[g, weight_rows(far)])

        lax.fori_loop(0, 3, gate, None)

    def cells(it, p, carry):
        def visit(k, carry):
            run_a, run_b, err = carry
            j = p * group + k
            at = pl.ds(pl.multiple_of(j * SEGS, SEGS), SEGS)
            prev, state = hist[j], hist[j + 1]
            zeta = sigmoid(acc[0, at] + inp[0, at])
            reset = sigmoid(acc[1, at] + inp[1, at])
            cand_pre = acc[2, at] + hb_ref[...]
            cand = jnp.tanh(inp[2, at] + reset * cand_pre)
            moved = zeta * (prev - cand)
            value = cand + moved
            slope = reset * (diag[2] + cand_pre * (1.0 - reset) * diag[1])
            slope = moved * diag[0] + (1.0 - cand * cand) * slope
            slope = zeta + (1.0 - zeta) * slope
            gap = state - value
            run_a = slope * run_a
            run_b = slope * run_b + (value - slope * prev)
            pre_a[j] = run_a
            pre_b[j] = run_b
            return run_a, run_b, err + gap * gap

        return lax.fori_loop(0, group, visit, carry, unroll=2)

    def sweep(it):
        near_products(it)
        carry = (
            jnp.ones((SEGS, width), F32),
            jnp.zeros((SEGS, width), F32),
            jnp.zeros((SEGS, width), F32),
        )
        far_products(it, ORDER[0])
        far_products(it, ORDER[1])
        carry = cells(it, 0, carry)
        carry = cells(it, 1, carry)
        far_products(it, 2)
        carry = cells(it, 2, carry)
        far_products(it, 3)
        return cells(it, 3, carry)

    def line_copy(it, k):
        return pltpu.make_async_remote_copy(
            src_ref=line_maps.at[it, mine],
            dst_ref=line_maps.at[it, mine],
            send_sem=line_sem.at[it, 0],
            recv_sem=line_sem.at[it, 1],
            device_id=line_peer(k),
            device_id_type=MESH,
        )

    def x_copy(it, k):
        return pltpu.make_async_remote_copy(
            src_ref=x_maps.at[it, x],
            dst_ref=x_maps.at[it, x],
            send_sem=x_sem.at[it, 0],
            recv_sem=x_sem.at[it, 1],
            device_id={"tm_0": lax.rem(x + k, nx)},
            device_id_type=MESH,
        )

    def res_copy(k):
        return pltpu.make_async_remote_copy(
            src_ref=line_res.at[mine],
            dst_ref=line_res.at[mine],
            send_sem=res_sem.at[0],
            recv_sem=res_sem.at[1],
            device_id=line_peer(k),
            device_id_type=MESH,
        )

    def plane_copy(k):
        return pltpu.make_async_remote_copy(
            src_ref=plane_res.at[x * ny + y],
            dst_ref=plane_res.at[x * ny + y],
            send_sem=res_sem.at[2],
            recv_sem=res_sem.at[3],
            device_id=plane_peer(k),
            device_id_type=MESH,
        )

    def start(copy, k):
        copy(k).start()

    def entering(it, run_a, run_b, sums):
        map_a, map_b = jnp.ones((1, width), F32), jnp.zeros((1, width), F32)
        for s in range(SEGS):
            seg[0, s : s + 1] = map_a
            seg[1, s : s + 1] = map_b
            map_b = run_a[s : s + 1] * map_b + run_b[s : s + 1]
            map_a = run_a[s : s + 1] * map_a
        line_maps[it, mine] = jnp.concatenate([lanes_to_rows(map_a), lanes_to_rows(map_b)], 0)
        lax.fori_loop(1, members, lambda k, _: start(functools.partial(line_copy, it), k), None)
        if sums is not None:
            line_res[mine] = jnp.concatenate([jnp.sum(e, 0, keepdims=True) for e in sums], 0)
            lax.fori_loop(1, members, lambda k, _: start(res_copy, k), None)
        wait_bytes(line_maps.at[it, pl.ds(0, members - 1)], line_sem.at[it, 1])
        all_a, all_b = jnp.ones((tiles, LANES), F32), jnp.zeros((tiles, LANES), F32)
        own_a, own_b = all_a, all_b
        for k in range(members):
            step_a, step_b = line_maps[it, k, 0:tiles], line_maps[it, k, tiles : 2 * tiles]
            all_b = step_a * all_b + step_b
            all_a = step_a * all_a
            own_a = jnp.where(mine == k + 1, all_a, own_a)
            own_b = jnp.where(mine == k + 1, all_b, own_b)
        x_maps[it, x] = jnp.concatenate([all_a, all_b], 0)
        lax.fori_loop(1, nx, lambda k, _: start(functools.partial(x_copy, it), k), None)
        if sums is not None:
            wait_bytes(line_res.at[pl.ds(0, members - 1)], res_sem.at[1])
            plane_res[x * ny + y] = functools.reduce(
                jnp.add, [line_res[k] for k in range(members)]
            )
            lax.fori_loop(1, plane, lambda k, _: start(plane_copy, k), None)
        wait_bytes(x_maps.at[it, pl.ds(0, nx - 1)], x_sem.at[it, 1])
        held = lanes_to_rows(init_ref[...])
        for k in range(nx):
            step_a, step_b = x_maps[it, k, 0:tiles], x_maps[it, k, tiles : 2 * tiles]
            held = jnp.where(k < x, step_a * held + step_b, held)
        held = rows_to_lanes(own_a * held + own_b)
        return seg[0] * held + seg[1]

    def apply(p, enter):
        at = pl.ds(p * group, group)
        hist[pl.ds(1 + p * group, group)] = pre_a[at] * enter + pre_b[at]

    send_block(0, ORDER[0])
    table_copy.start()
    weight_copy.start()
    edge_copy.wait()
    first = lax.broadcasted_iota(jnp.int32, (SEGS, width), 0) == 0
    outer = jnp.where(tm == 0, jnp.broadcast_to(init_ref[...], (SEGS, width)), pltpu.roll(edge[...], 1, 0))
    hist[0] = jnp.where(first, outer, pltpu.roll(hist[steps], 1, 0))
    send_block(0, ORDER[1])
    send_block(0, 2)
    send_block(0, 3)

    table_copy.wait()

    def split(g, _):
        rest = table[g]
        for k in range(3):
            part = rest.astype(BF16)
            pieces[k, g] = part
            rest = rest - part.astype(F32)

    lax.fori_loop(0, 3, split, None)
    lane = lax.broadcasted_iota(jnp.int32, (SEGS, vocab), 1)

    def mark(k, _):
        ids = pltpu.roll(ids_ref[...], lax.rem(LANES - k * 8, LANES), 1)
        for u in range(0, 8, 2):
            both = [jnp.where(ids[:, v : v + 1] == lane, 1.0, 0.0) for v in (u, u + 1)]
            at = pl.ds(pl.multiple_of((k * 8 + u) * SEGS, 2 * SEGS), 2 * SEGS)
            onehot[at] = jnp.concatenate(both, 0).astype(BF16)

    lax.fori_loop(0, steps // 8, mark, None)

    def look_up(p, _):
        for g in range(3):
            found = dot(onehot[block_rows(p)], pieces[0, g])
            found += dot(onehot[block_rows(p)], pieces[1, g])
            found += dot(onehot[block_rows(p)], pieces[2, g])
            if g == 0:
                found += zb_ref[...]
            inp[g, block_rows(p)] = found

    lax.fori_loop(0, PAIRS, look_up, None)

    weight_copy.wait()
    same = lax.broadcasted_iota(jnp.int32, (LANES, LANES), 0) == lax.broadcasted_iota(
        jnp.int32, (LANES, LANES), 1
    )
    for g in range(3):
        for k in range(tiles):
            at = pl.ds(pl.multiple_of(y * width + k * LANES, LANES), LANES)
            corner = weight[g, at, k * LANES : (k + 1) * LANES].astype(F32)
            line = jnp.sum(jnp.where(same, corner, 0.0), 0, keepdims=True)
            diag[g, :, k * LANES : (k + 1) * LANES] = jnp.broadcast_to(line, (SEGS, LANES))

    run_a, run_b, first_err = sweep(0)
    enter = entering(0, run_a, run_b, None)
    hist[0] = enter
    for p in ORDER[:2][::-1]:
        apply(p, enter)
    for p in ORDER:
        if p > 1:
            apply(p, enter)
        send_block(1, p)
    first_sum = sum_tiles(first_err)

    run_a, run_b, second_err = sweep(1)
    second_sum = sum_tiles(second_err)
    enter = entering(1, run_a, run_b, (first_sum, second_sum))

    def out_copy(p, s):
        return pltpu.make_async_copy(
            hist.at[pl.ds(1 + p * group, group), s],
            out_hbm.at[pl.ds(s * steps + p * group, group)],
            out_sem.at[p, s],
        )

    for p in range(PAIRS):
        apply(p, enter)
        for s in range(SEGS):
            out_copy(p, s).start()
    wait_bytes(plane_res.at[pl.ds(0, plane - 1)], res_sem.at[3])
    sums = functools.reduce(jnp.add, [plane_res[k] for k in range(plane)])
    norms = jnp.sqrt(jnp.sum(sums, 1, keepdims=True) / count)
    for it in range(ITERS):
        res_ref[it] = norms[it, 0]

    for it in range(ITERS):
        wait_bytes(sent.at[it, pl.ds(0, 3)], send_sem.at[it])
        wait_bytes(line_maps.at[it, pl.ds(0, members - 1)], line_sem.at[it, 0])
        wait_bytes(x_maps.at[it, pl.ds(0, nx - 1)], x_sem.at[it, 0])
    wait_bytes(line_res.at[pl.ds(0, members - 1)], res_sem.at[0])
    wait_bytes(plane_res.at[pl.ds(0, plane - 1)], res_sem.at[2])
    for p in range(PAIRS):
        for s in range(SEGS):
            out_copy(p, s).wait()


def sum_tiles(err):
    return functools.reduce(
        jnp.add, [err[:, k : k + LANES] for k in range(0, err.shape[1], LANES)]
    )


def per_device(token_ids, input_table, recur_weight, z_bias, hn_bias, init_state, guess):
    rows, width = guess.shape
    vocab, full = input_table.shape[0], recur_weight.shape[0]
    nx, nz, nc, ny = (lax.axis_size(a) for a in (*TM, "hid"))
    steps, members, plane, tiles = rows // SEGS, nz * nc, nx * ny, width // LANES
    group = steps // PAIRS
    ids = token_ids.reshape(SEGS, steps)
    ids = jnp.concatenate([ids] * (LANES // steps), 1)
    anywhere = pl.BlockSpec(memory_space=pl.ANY)
    vmem = pl.BlockSpec(memory_space=pltpu.VMEM)
    sem = pltpu.SemaphoreType.DMA
    return pl.pallas_call(
        functools.partial(kernel, (nx, nz, nc, ny, rows, width, vocab)),
        out_shape=(
            jax.ShapeDtypeStruct((rows, width), F32),
            jax.ShapeDtypeStruct((ITERS,), F32),
        ),
        in_specs=[vmem, anywhere, anywhere, vmem, vmem, vmem, anywhere],
        out_specs=(anywhere, pl.BlockSpec(memory_space=pltpu.SMEM)),
        scratch_shapes=[
            pltpu.VMEM((3, vocab, width), F32),
            pltpu.VMEM((3, 3, vocab, width), BF16),
            pltpu.VMEM((3, full, width), BF16),
            pltpu.VMEM((steps + 1, SEGS, width), F32),
            pltpu.VMEM((ITERS, ny, rows, width), BF16),
            pltpu.VMEM((rows, vocab), BF16),
            pltpu.VMEM((3, rows, width), F32),
            pltpu.VMEM((3, rows, width), F32),
            pltpu.VMEM((steps, SEGS, width), F32),
            pltpu.VMEM((steps, SEGS, width), F32),
            pltpu.VMEM((3, SEGS, width), F32),
            pltpu.VMEM((2, SEGS, width), F32),
            pltpu.VMEM((SEGS, width), F32),
            pltpu.VMEM((ITERS, members, 2 * tiles, LANES), F32),
            pltpu.VMEM((ITERS, nx, 2 * tiles, LANES), F32),
            pltpu.VMEM((members, ITERS, LANES), F32),
            pltpu.VMEM((plane, ITERS, LANES), F32),
            sem((SEGS,)),
            sem((2,)),
            sem((PAIRS, SEGS)),
            sem((2,)),
            sem((ITERS,)),
            sem((ITERS, 2, PAIRS)),
            sem((ITERS, 2, PAIRS)),
            sem((ITERS, 2)),
            sem((ITERS, 2)),
            sem((4,)),
        ],
        compiler_params=pltpu.CompilerParams(
            collective_id=0, has_side_effects=True, vmem_limit_bytes=60 * 1024 * 1024
        ),
    )(
        ids,
        jnp.transpose(input_table, (1, 0, 2)),
        jnp.transpose(recur_weight, (1, 0, 2)),
        z_bias[None],
        hn_bias[None],
        init_state[None],
        guess,
    )


def solution(mesh):
    chips = mesh.devices.shape[0]
    nz, nc = (8, 2) if chips == 64 else (2, 2)
    finer = Mesh(
        mesh.devices.reshape(chips // (nz * nc), nz, nc, mesh.shape["hid"]), (*TM, "hid")
    )
    in_specs = (
        P(TM),
        P(None, None, "hid"),
        P(None, None, "hid"),
        P("hid"),
        P("hid"),
        P("hid"),
        P(TM, "hid"),
    )
    return jax.shard_map(
        per_device, mesh=finer, in_specs=in_specs, out_specs=(P(TM, "hid"), P()), check_vma=False
    )
```

profile of v0, /device:TPU:1, one launch (start us, length us, event | category | flops | bytes accessed | tf_op | source)
XLA Modules:
  0.0 78.2 jit_solution(3994685979276888083)
XLA Ops:
  0.6 0.8 reshape.7
  1.4 0.7 pad_add_fusion.ids_ref
  2.1 72.7 %shard_map.86 = (f32[512,512]{1,0:T(8,128)}, f32[2]{0:T(128)}) custom-call(s32[8,128]{1,0:T(8,128)} %pad_add_fusion.ids_ref, f32[3,256,512]{2,1,0:T(8,128)} %bitcast.6, bf16[3,2048,512]{2,1,0:T(8,128)(2,1)} %bitcast.5, f32[1,512]{1,0:T(1,128)} %bitcast.7, f32[1,512]{1,0:T(1,128)} %bitcast.8, f32[1,512]{1,0:T(1,128)} %bitcast.9, f32[512,512]{1,0:T(8,128)} %guess_hbm.1), custom_call_target="tpu_custom_call" | custom-call | tf_op jit(solution)/shard_map/pallas_call | solution.py:446
  74.8 2.3 %copy.11 = f32[512,512]{1,0:T(8,128)} copy(f32[512,512]{1,0:T(8,128)} %get-tuple-element.4) | data formatting | bytes 2097152
  77.1 1.1 %copy.12 = f32[2]{0:T(128)} copy(f32[2]{0:T(128)} %get-tuple-element.5) | data formatting | bytes 16
where the time goes:
time: 78.4 us; the launch traced here: 78.2 us
  Pallas kernels  72.7 us (93%)
  local copies, waits for them, and re-layouts  4.13 us (5%)
    pallas_call x1, Pallas kernels, per_device(): pl.pallas_call(functools.partial(kernel, (nx, nz, nc, ny, rows, width, vo...  72.7 us
    unnamed x2, local copies, waits for them, and re-layouts  3.38 us

commit v1 on v0

--- a/solution.py
+++ b/solution.py
@@ -41,19 +41,22 @@
 
 def kernel(
     dims,
-    ids_ref,
+    ids_hbm,
     table_hbm,
     weight_hbm,
+    zb_hbm,
+    hb_hbm,
+    init_hbm,
+    guess_hbm,
+    hist,
+    plane_res,
+    ids_ref,
     zb_ref,
     hb_ref,
     init_ref,
-    guess_hbm,
-    out_hbm,
-    res_ref,
     table,
     pieces,
     weight,
-    hist,
     sent,
     onehot,
     inp,
@@ -66,10 +69,8 @@
     line_maps,
     x_maps,
     line_res,
-    plane_res,
     in_sem,
     weight_sem,
-    out_sem,
     edge_sem,
     send_sem,
     recv_sem,
@@ -89,9 +90,9 @@
     mine = z * nc + c
     tm = x * members + mine
     right, left, far = (lax.rem(y + d, ny) for d in (1, ny - 1, 2))
-    count = nx * members * rows * ny * width
 
     def line_peer(k):
+        k = members // 2 + k // 2 * (1 - 2 * lax.rem(k, 2))
         peer = lax.rem(mine + k, members)
         return {"tm_1": peer // nc, "tm_2": lax.rem(peer, nc)}
 
@@ -126,6 +127,14 @@
         pltpu.make_async_copy(
             guess_hbm.at[pl.ds(s * steps, steps)], hist.at[pl.ds(1, steps), s], in_sem.at[s]
         ).wait()
+    rows_copies = [
+        pltpu.make_async_copy(source, target, in_sem.at[SEGS + k])
+        for k, (source, target) in enumerate(
+            ((ids_hbm, ids_ref), (zb_hbm, zb_ref), (hb_hbm, hb_ref), (init_hbm, init_ref))
+        )
+    ]
+    for copy in rows_copies:
+        copy.start()
     table_copy = pltpu.make_async_copy(table_hbm, table, weight_sem.at[0])
     weight_copy = pltpu.make_async_copy(weight_hbm, weight, weight_sem.at[1])
     pl.semaphore_wait(barrier, plane + members)
@@ -289,6 +298,9 @@
         copy(k).start()
 
     def entering(it, run_a, run_b, sums):
+        if sums is not None:
+            line_res[mine] = jnp.concatenate([jnp.sum(e, 0, keepdims=True) for e in sums], 0)
+            lax.fori_loop(1, members, lambda k, _: start(res_copy, k), None)
         map_a, map_b = jnp.ones((1, width), F32), jnp.zeros((1, width), F32)
         for s in range(SEGS):
             seg[0, s : s + 1] = map_a
@@ -297,9 +309,6 @@
             map_a = run_a[s : s + 1] * map_a
         line_maps[it, mine] = jnp.concatenate([lanes_to_rows(map_a), lanes_to_rows(map_b)], 0)
         lax.fori_loop(1, members, lambda k, _: start(functools.partial(line_copy, it), k), None)
-        if sums is not None:
-            line_res[mine] = jnp.concatenate([jnp.sum(e, 0, keepdims=True) for e in sums], 0)
-            lax.fori_loop(1, members, lambda k, _: start(res_copy, k), None)
         wait_bytes(line_maps.at[it, pl.ds(0, members - 1)], line_sem.at[it, 1])
         all_a, all_b = jnp.ones((tiles, LANES), F32), jnp.zeros((tiles, LANES), F32)
         own_a, own_b = all_a, all_b
@@ -332,6 +341,8 @@
     send_block(0, ORDER[0])
     table_copy.start()
     weight_copy.start()
+    for copy in rows_copies:
+        copy.wait()
     edge_copy.wait()
     first = lax.broadcasted_iota(jnp.int32, (SEGS, width), 0) == 0
     outer = jnp.where(tm == 0, jnp.broadcast_to(init_ref[...], (SEGS, width)), pltpu.roll(edge[...], 1, 0))
@@ -351,9 +362,16 @@
 
     lax.fori_loop(0, 3, split, None)
     lane = lax.broadcasted_iota(jnp.int32, (SEGS, vocab), 1)
+    lines = []
+    for s in range(SEGS):
+        tile = s * steps // LANES * LANES
+        line = ids_ref[:, tile : tile + LANES]
+        back = s * steps - tile
+        lines.append(pltpu.roll(line, LANES - back, 1) if back else line)
+    by_segment = jnp.concatenate(lines, 0)
 
     def mark(k, _):
-        ids = pltpu.roll(ids_ref[...], lax.rem(LANES - k * 8, LANES), 1)
+        ids = pltpu.roll(by_segment, lax.rem(LANES - k * 8, LANES), 1)
         for u in range(0, 8, 2):
             both = [jnp.where(ids[:, v : v + 1] == lane, 1.0, 0.0) for v in (u, u + 1)]
             at = pl.ds(pl.multiple_of((k * 8 + u) * SEGS, 2 * SEGS), 2 * SEGS)
@@ -398,22 +416,9 @@
     second_sum = sum_tiles(second_err)
     enter = entering(1, run_a, run_b, (first_sum, second_sum))
 
-    def out_copy(p, s):
-        return pltpu.make_async_copy(
-            hist.at[pl.ds(1 + p * group, group), s],
-            out_hbm.at[pl.ds(s * steps + p * group, group)],
-            out_sem.at[p, s],
-        )
-
     for p in range(PAIRS):
         apply(p, enter)
-        for s in range(SEGS):
-            out_copy(p, s).start()
     wait_bytes(plane_res.at[pl.ds(0, plane - 1)], res_sem.at[3])
-    sums = functools.reduce(jnp.add, [plane_res[k] for k in range(plane)])
-    norms = jnp.sqrt(jnp.sum(sums, 1, keepdims=True) / count)
-    for it in range(ITERS):
-        res_ref[it] = norms[it, 0]
 
     for it in range(ITERS):
         wait_bytes(sent.at[it, pl.ds(0, 3)], send_sem.at[it])
@@ -421,9 +426,24 @@
         wait_bytes(x_maps.at[it, pl.ds(0, nx - 1)], x_sem.at[it, 0])
     wait_bytes(line_res.at[pl.ds(0, members - 1)], res_sem.at[0])
     wait_bytes(plane_res.at[pl.ds(0, plane - 1)], res_sem.at[2])
-    for p in range(PAIRS):
-        for s in range(SEGS):
-            out_copy(p, s).wait()
+
+
+def write_out(count, hist, plane_res, out_hbm, res_ref, out_sem):
+    steps = hist.shape[0] - 1
+    copies = [
+        pltpu.make_async_copy(
+            hist.at[pl.ds(1, steps), s], out_hbm.at[pl.ds(s * steps, steps)], out_sem.at[s]
+        )
+        for s in range(SEGS)
+    ]
+    for copy in copies:
+        copy.start()
+    sums = functools.reduce(jnp.add, [plane_res[k] for k in range(plane_res.shape[0])])
+    norms = jnp.sqrt(jnp.sum(sums, 1, keepdims=True) / count)
+    for it in range(ITERS):
+        res_ref[it] = norms[it, 0]
+    for copy in copies:
+        copy.wait()
 
 
 def sum_tiles(err):
@@ -438,24 +458,25 @@
     nx, nz, nc, ny = (lax.axis_size(a) for a in (*TM, "hid"))
     steps, members, plane, tiles = rows // SEGS, nz * nc, nx * ny, width // LANES
     group = steps // PAIRS
-    ids = token_ids.reshape(SEGS, steps)
-    ids = jnp.concatenate([ids] * (LANES // steps), 1)
     anywhere = pl.BlockSpec(memory_space=pl.ANY)
     vmem = pl.BlockSpec(memory_space=pltpu.VMEM)
     sem = pltpu.SemaphoreType.DMA
-    return pl.pallas_call(
+    hist, plane_res = pl.pallas_call(
         functools.partial(kernel, (nx, nz, nc, ny, rows, width, vocab)),
         out_shape=(
-            jax.ShapeDtypeStruct((rows, width), F32),
-            jax.ShapeDtypeStruct((ITERS,), F32),
+            pltpu.VMEM((steps + 1, SEGS, width), F32),
+            pltpu.VMEM((plane, ITERS, LANES), F32),
         ),
-        in_specs=[vmem, anywhere, anywhere, vmem, vmem, vmem, anywhere],
-        out_specs=(anywhere, pl.BlockSpec(memory_space=pltpu.SMEM)),
+        in_specs=[pl.BlockSpec(memory_space=pltpu.HBM)] * 7,
+        out_specs=(vmem, vmem),
         scratch_shapes=[
+            pltpu.VMEM((1, rows), jnp.int32),
+            pltpu.VMEM((1, width), F32),
+            pltpu.VMEM((1, width), F32),
+            pltpu.VMEM((1, width), F32),
             pltpu.VMEM((3, vocab, width), F32),
             pltpu.VMEM((3, 3, vocab, width), BF16),
             pltpu.VMEM((3, full, width), BF16),
-            pltpu.VMEM((steps + 1, SEGS, width), F32),
             pltpu.VMEM((ITERS, ny, rows, width), BF16),
             pltpu.VMEM((rows, vocab), BF16),
             pltpu.VMEM((3, rows, width), F32),
@@ -468,10 +489,8 @@
             pltpu.VMEM((ITERS, members, 2 * tiles, LANES), F32),
             pltpu.VMEM((ITERS, nx, 2 * tiles, LANES), F32),
             pltpu.VMEM((members, ITERS, LANES), F32),
-            pltpu.VMEM((plane, ITERS, LANES), F32),
-            sem((SEGS,)),
+            sem((SEGS + 4,)),
             sem((2,)),
-            sem((PAIRS, SEGS)),
             sem((2,)),
             sem((ITERS,)),
             sem((ITERS, 2, PAIRS)),
@@ -481,17 +500,33 @@
             sem((4,)),
         ],
         compiler_params=pltpu.CompilerParams(
-            collective_id=0, has_side_effects=True, vmem_limit_bytes=60 * 1024 * 1024
+            collective_id=0, has_side_effects=True, vmem_limit_bytes=40 * 1024 * 1024
         ),
     )(
-        ids,
-        jnp.transpose(input_table, (1, 0, 2)),
-        jnp.transpose(recur_weight, (1, 0, 2)),
-        z_bias[None],
-        hn_bias[None],
-        init_state[None],
-        guess,
-    )
+        *(
+            pltpu.with_memory_space_constraint(array, pltpu.HBM)
+            for array in (
+                token_ids[None],
+                jnp.transpose(input_table, (1, 0, 2)),
+                jnp.transpose(recur_weight, (1, 0, 2)),
+                z_bias[None],
+                hn_bias[None],
+                init_state[None],
+                guess,
+            )
+        )
+    )
+    return pl.pallas_call(
+        functools.partial(write_out, nx * members * rows * ny * width),
+        out_shape=(
+            jax.ShapeDtypeStruct((rows, width), F32),
+            jax.ShapeDtypeStruct((ITERS,), F32),
+        ),
+        in_specs=[vmem, vmem],
+        out_specs=(anywhere, pl.BlockSpec(memory_space=pltpu.SMEM)),
+        scratch_shapes=[sem((SEGS,))],
+        compiler_params=pltpu.CompilerParams(vmem_limit_bytes=8 * 1024 * 1024),
+    )(hist, plane_res)
 
 
 def solution(mesh):

time: 78.4 us -> 73.4 us (0.936)
  local copies, waits for them, and re-layouts: 4.13 us -> 0 us
    unnamed x2 -> x0, local copies, waits for them, and re-layouts: 3.38 us -> none
    pallas_call x1, Pallas kernels: 72.7 us -> 71 us  [per_device(): pl.pallas_call(functools.partial(kernel, (nx, nz, nc, ny, rows, width, vo...]
    pallas_call x0 -> x1, Pallas kernels: none -> 1.55 us  [per_device(): pl.pallas_call(functools.partial(write_out, nx * members * rows * ny * wi...]
where the time goes in v1:
time: 73.4 us; the launch traced here: 73.2 us
  Pallas kernels  72.6 us (99%)
    pallas_call x1, Pallas kernels, per_device(): pl.pallas_call(functools.partial(kernel, (nx, nz, nc, ny, rows, width, vo...  71 us
    pallas_call x1, Pallas kernels, per_device(): pl.pallas_call(functools.partial(write_out, nx * members * rows * ny * wi...  1.55 us

profile of v1, /device:TPU:1, one launch (start us, length us, event | category | flops | bytes accessed | tf_op | source)
XLA Modules:
  0.0 73.2 jit_solution(7795281894532196193)
XLA Ops:
  0.6 71.0 %shard_map.86 = (f32[65,8,512]{2,1,0:T(8,128)S(1)}, f32[16,2,128]{2,1,0:T(2,128)S(1)}) custom-call(s32[1,512]{1,0:T(1,128)} %bitcast.8, f32[3,256,512]{2,1,0:T(8,128)} %bitcast.7, bf16[3,2048,512]{2,1,0:T(8,128)(2,1)} %bitcast.6, f32[1,512]{1,0:T(1,128)} %bitcast.9, f32[1,512]{1,0:T(1,128)} %bitcast.10, f32[1,512]{1,0:T(1,128)} %bitcast.11, f32[512,512]{1,0:T(8,128)} %guess_hbm.1), custom_call_target="tpu_custom_call" | custom-call | tf_op jit(solution)/shard_map/pallas_call | solution.py:464
  71.7 1.5 %shard_map.87 = (f32[512,512]{1,0:T(8,128)}, f32[2]{0:T(128)}) custom-call(f32[65,8,512]{2,1,0:T(8,128)S(1)} %get-tuple-element.4.hist, f32[16,2,128]{2,1,0:T(2,128)S(1)} %get-tuple-element.5.plane_res), custom_call_target="tpu_custom_call" | custom-call | tf_op jit(solution)/shard_map/pallas_call | solution.py:519

commit v2 on v1

--- a/solution.py
+++ b/solution.py
@@ -12,7 +12,7 @@
 SEGS = 8
 PAIRS = 4
 LANES = 128
-ORDER = (1, 0, 2, 3)
+ORDERS = ((1, 0, 2, 3), (0, 1, 2, 3))
 TM = ("tm_0", "tm_1", "tm_2")
 MESH = pl.DeviceIdType.MESH
 F32 = jnp.float32
@@ -49,7 +49,7 @@
     init_hbm,
     guess_hbm,
     hist,
-    plane_res,
+    sums_ref,
     ids_ref,
     zb_ref,
     hb_ref,
@@ -66,17 +66,27 @@
     diag,
     seg,
     edge,
-    line_maps,
+    own_map,
+    twin_map,
+    z_maps,
     x_maps,
-    line_res,
+    enter_row,
+    here,
+    own_res,
+    twin_res,
+    z_res,
+    plane_res,
+    sum_row,
     in_sem,
     weight_sem,
     edge_sem,
     send_sem,
     recv_sem,
     relay_sem,
-    line_sem,
+    map_sem,
+    z_sem,
     x_sem,
+    enter_sem,
     res_sem,
 ):
     nx, nz, nc, ny, rows, width, vocab = dims
@@ -87,14 +97,21 @@
     members = nz * nc
     plane = nx * ny
     x, z, c, y = (lax.axis_index(a) for a in (*TM, "hid"))
-    mine = z * nc + c
-    tm = x * members + mine
+    tm = x * members + z * nc + c
+    twin = {"tm_2": 1 - c}
     right, left, far = (lax.rem(y + d, ny) for d in (1, ny - 1, 2))
 
-    def line_peer(k):
-        k = members // 2 + k // 2 * (1 - 2 * lax.rem(k, 2))
-        peer = lax.rem(mine + k, members)
-        return {"tm_1": peer // nc, "tm_2": lax.rem(peer, nc)}
+    def far_first(k, size):
+        return size // 2 + k // 2 * (1 - 2 * lax.rem(k, 2))
+
+    def z_peer(k):
+        return {"tm_1": lax.rem(z + far_first(k, nz), nz)}
+
+    def x_peer(k):
+        return {"tm_0": lax.rem(x + far_first(k, nx), nx)}
+
+    def each(count, act):
+        lax.fori_loop(1, count, lambda k, _: act(k), None)
 
     def plane_peer(k):
         return {"tm_0": lax.rem(x + k // ny, nx), "hid": lax.rem(y + lax.rem(k, ny), ny)}
@@ -116,8 +133,9 @@
 
     greet(tm_peer(after))
     greet(tm_peer(before))
-    lax.fori_loop(1, plane, lambda k, _: greet(plane_peer(k)), None)
-    lax.fori_loop(1, members, lambda k, _: greet(line_peer(k)), None)
+    greet(twin)
+    each(plane, lambda k: greet(plane_peer(k)))
+    each(nz, lambda k: greet(z_peer(k)))
 
     for s in range(SEGS):
         pltpu.make_async_copy(
@@ -137,7 +155,7 @@
         copy.start()
     table_copy = pltpu.make_async_copy(table_hbm, table, weight_sem.at[0])
     weight_copy = pltpu.make_async_copy(weight_hbm, weight, weight_sem.at[1])
-    pl.semaphore_wait(barrier, plane + members)
+    pl.semaphore_wait(barrier, plane + nz + 1)
 
     edge_copy = pltpu.make_async_remote_copy(
         src_ref=hist.at[steps],
@@ -189,7 +207,7 @@
 
     def near_products(it):
         def visit(i, _):
-            p = jnp.where(i < 2, 1 - i, i)
+            p = jnp.where(i < 2, 1 - i, i) if it == 0 else i
             direct(it, p, 0, left).wait_recv()
             relay(it, p, 0, left).start()
             direct(it, p, 1, right).wait_recv()
@@ -209,10 +227,8 @@
         relay(it, p, 0, far).wait_recv()
         relay(it, p, 1, far).wait_recv()
 
-        def gate(g, _):
+        for g in range(3):
             acc[g, block_rows(p)] += dot(sent[it, far, block_rows(p)], weight[g, weight_rows(far)])
-
-        lax.fori_loop(0, 3, gate, None)
 
     def cells(it, p, carry):
         def visit(k, carry):
@@ -245,100 +261,117 @@
             jnp.zeros((SEGS, width), F32),
             jnp.zeros((SEGS, width), F32),
         )
-        far_products(it, ORDER[0])
-        far_products(it, ORDER[1])
-        carry = cells(it, 0, carry)
-        carry = cells(it, 1, carry)
-        far_products(it, 2)
-        carry = cells(it, 2, carry)
-        far_products(it, 3)
-        return cells(it, 3, carry)
-
-    def line_copy(it, k):
+        ready = 0
+        for i, p in enumerate(ORDERS[it]):
+            far_products(it, p)
+            while ready in ORDERS[it][: i + 1]:
+                carry = cells(it, ready, carry)
+                ready += 1
+        return carry
+
+    def send(ref, target, sems, peer):
         return pltpu.make_async_remote_copy(
-            src_ref=line_maps.at[it, mine],
-            dst_ref=line_maps.at[it, mine],
-            send_sem=line_sem.at[it, 0],
-            recv_sem=line_sem.at[it, 1],
-            device_id=line_peer(k),
+            src_ref=ref,
+            dst_ref=target,
+            send_sem=sems.at[0],
+            recv_sem=sems.at[1],
+            device_id=peer,
             device_id_type=MESH,
         )
 
+    def map_copy(it):
+        return send(own_map.at[it], twin_map.at[it], map_sem.at[it], twin)
+
+    def z_copy(it, k):
+        return send(z_maps.at[it, z], z_maps.at[it, z], z_sem.at[it], z_peer(k))
+
     def x_copy(it, k):
-        return pltpu.make_async_remote_copy(
-            src_ref=x_maps.at[it, x],
-            dst_ref=x_maps.at[it, x],
-            send_sem=x_sem.at[it, 0],
-            recv_sem=x_sem.at[it, 1],
-            device_id={"tm_0": lax.rem(x + k, nx)},
-            device_id_type=MESH,
-        )
-
-    def res_copy(k):
-        return pltpu.make_async_remote_copy(
-            src_ref=line_res.at[mine],
-            dst_ref=line_res.at[mine],
-            send_sem=res_sem.at[0],
-            recv_sem=res_sem.at[1],
-            device_id=line_peer(k),
-            device_id_type=MESH,
-        )
+        return send(x_maps.at[it, x], x_maps.at[it, x], x_sem.at[it], x_peer(k))
+
+    def enter_copy(it):
+        return send(enter_row.at[it], enter_row.at[it], enter_sem.at[it], twin)
+
+    def twin_res_copy():
+        return send(own_res, twin_res, res_sem.at[0], twin)
+
+    def z_res_copy(k):
+        return send(z_res.at[z], z_res.at[z], res_sem.at[1], z_peer(k))
 
     def plane_copy(k):
-        return pltpu.make_async_remote_copy(
-            src_ref=plane_res.at[x * ny + y],
-            dst_ref=plane_res.at[x * ny + y],
-            send_sem=res_sem.at[2],
-            recv_sem=res_sem.at[3],
-            device_id=plane_peer(k),
-            device_id_type=MESH,
-        )
-
-    def start(copy, k):
-        copy(k).start()
+        slot = plane_res.at[x * ny + y]
+        return send(slot, slot, res_sem.at[2], plane_peer(k))
+
+    def sum_copy():
+        return send(sum_row, sum_row, res_sem.at[3], twin)
+
+    def halves(block):
+        return block[0:tiles], block[tiles : 2 * tiles]
 
     def entering(it, run_a, run_b, sums):
         if sums is not None:
-            line_res[mine] = jnp.concatenate([jnp.sum(e, 0, keepdims=True) for e in sums], 0)
-            lax.fori_loop(1, members, lambda k, _: start(res_copy, k), None)
+            own_res[...] = jnp.concatenate([jnp.sum(e, 0, keepdims=True) for e in sums], 0)
+
+            @pl.when(c == 0)
+            def _():
+                twin_res_copy().start()
+
         map_a, map_b = jnp.ones((1, width), F32), jnp.zeros((1, width), F32)
         for s in range(SEGS):
             seg[0, s : s + 1] = map_a
             seg[1, s : s + 1] = map_b
             map_b = run_a[s : s + 1] * map_b + run_b[s : s + 1]
             map_a = run_a[s : s + 1] * map_a
-        line_maps[it, mine] = jnp.concatenate([lanes_to_rows(map_a), lanes_to_rows(map_b)], 0)
-        lax.fori_loop(1, members, lambda k, _: start(functools.partial(line_copy, it), k), None)
-        wait_bytes(line_maps.at[it, pl.ds(0, members - 1)], line_sem.at[it, 1])
-        all_a, all_b = jnp.ones((tiles, LANES), F32), jnp.zeros((tiles, LANES), F32)
-        own_a, own_b = all_a, all_b
-        for k in range(members):
-            step_a, step_b = line_maps[it, k, 0:tiles], line_maps[it, k, tiles : 2 * tiles]
-            all_b = step_a * all_b + step_b
-            all_a = step_a * all_a
-            own_a = jnp.where(mine == k + 1, all_a, own_a)
-            own_b = jnp.where(mine == k + 1, all_b, own_b)
-        x_maps[it, x] = jnp.concatenate([all_a, all_b], 0)
-        lax.fori_loop(1, nx, lambda k, _: start(functools.partial(x_copy, it), k), None)
-        if sums is not None:
-            wait_bytes(line_res.at[pl.ds(0, members - 1)], res_sem.at[1])
-            plane_res[x * ny + y] = functools.reduce(
-                jnp.add, [line_res[k] for k in range(members)]
-            )
-            lax.fori_loop(1, plane, lambda k, _: start(plane_copy, k), None)
-        wait_bytes(x_maps.at[it, pl.ds(0, nx - 1)], x_sem.at[it, 1])
-        held = lanes_to_rows(init_ref[...])
-        for k in range(nx):
-            step_a, step_b = x_maps[it, k, 0:tiles], x_maps[it, k, tiles : 2 * tiles]
-            held = jnp.where(k < x, step_a * held + step_b, held)
-        held = rows_to_lanes(own_a * held + own_b)
-        return seg[0] * held + seg[1]
+        own_map[it] = jnp.concatenate([lanes_to_rows(map_a), lanes_to_rows(map_b)], 0)
+
+        @pl.when(c == 0)
+        def _():
+            map_copy(it).start()
+            enter_copy(it).wait_recv()
+            here[...] = enter_row[it]
+
+        @pl.when(c == 1)
+        def _():
+            map_copy(it).wait_recv()
+            twin_a, twin_b = halves(twin_map[it])
+            last_a, last_b = halves(own_map[it])
+            z_maps[it, z] = jnp.concatenate([last_a * twin_a, last_a * twin_b + last_b], 0)
+            each(nz, lambda k: z_copy(it, k).start())
+            if sums is not None:
+                twin_res_copy().wait_recv()
+                z_res[z] = own_res[...] + twin_res[...]
+                each(nz, lambda k: z_res_copy(k).start())
+            wait_bytes(z_maps.at[it, pl.ds(0, nz - 1)], z_sem.at[it, 1])
+            all_a, all_b = jnp.ones((tiles, LANES), F32), jnp.zeros((tiles, LANES), F32)
+            own_a, own_b = all_a, all_b
+            for k in range(nz):
+                step_a, step_b = halves(z_maps[it, k])
+                all_b = step_a * all_b + step_b
+                all_a = step_a * all_a
+                own_a = jnp.where(z == k + 1, all_a, own_a)
+                own_b = jnp.where(z == k + 1, all_b, own_b)
+            x_maps[it, x] = jnp.concatenate([all_a, all_b], 0)
+            each(nx, lambda k: x_copy(it, k).start())
+            if sums is not None:
+                wait_bytes(z_res.at[pl.ds(0, nz - 1)], res_sem.at[1, 1])
+                plane_res[x * ny + y] = functools.reduce(jnp.add, [z_res[k] for k in range(nz)])
+                each(plane, lambda k: plane_copy(k).start())
+            wait_bytes(x_maps.at[it, pl.ds(0, nx - 1)], x_sem.at[it, 1])
+            held = lanes_to_rows(init_ref[...])
+            for k in range(nx):
+                step_a, step_b = halves(x_maps[it, k])
+                held = jnp.where(k < x, step_a * held + step_b, held)
+            held = own_a * held + own_b
+            enter_row[it] = held
+            enter_copy(it).start()
+            here[...] = twin_a * held + twin_b
+
+        return seg[0] * rows_to_lanes(here[...]) + seg[1]
 
     def apply(p, enter):
         at = pl.ds(p * group, group)
         hist[pl.ds(1 + p * group, group)] = pre_a[at] * enter + pre_b[at]
 
-    send_block(0, ORDER[0])
+    send_block(0, ORDERS[0][0])
     table_copy.start()
     weight_copy.start()
     for copy in rows_copies:
@@ -347,9 +380,8 @@
     first = lax.broadcasted_iota(jnp.int32, (SEGS, width), 0) == 0
     outer = jnp.where(tm == 0, jnp.broadcast_to(init_ref[...], (SEGS, width)), pltpu.roll(edge[...], 1, 0))
     hist[0] = jnp.where(first, outer, pltpu.roll(hist[steps], 1, 0))
-    send_block(0, ORDER[1])
-    send_block(0, 2)
-    send_block(0, 3)
+    for p in ORDERS[0][1:]:
+        send_block(0, p)
 
     table_copy.wait()
 
@@ -404,11 +436,8 @@
     run_a, run_b, first_err = sweep(0)
     enter = entering(0, run_a, run_b, None)
     hist[0] = enter
-    for p in ORDER[:2][::-1]:
+    for p in ORDERS[1]:
         apply(p, enter)
-    for p in ORDER:
-        if p > 1:
-            apply(p, enter)
         send_block(1, p)
     first_sum = sum_tiles(first_err)
 
@@ -418,17 +447,33 @@
 
     for p in range(PAIRS):
         apply(p, enter)
-    wait_bytes(plane_res.at[pl.ds(0, plane - 1)], res_sem.at[3])
-
+
+    @pl.when(c == 1)
+    def _():
+        wait_bytes(plane_res.at[pl.ds(0, plane - 1)], res_sem.at[2, 1])
+        sum_row[...] = functools.reduce(jnp.add, [plane_res[k] for k in range(plane)])
+        sum_copy().start()
+        for it in range(ITERS):
+            wait_bytes(z_maps.at[it, pl.ds(0, nz - 1)], z_sem.at[it, 0])
+            wait_bytes(x_maps.at[it, pl.ds(0, nx - 1)], x_sem.at[it, 0])
+            enter_copy(it).wait_send()
+        wait_bytes(z_res.at[pl.ds(0, nz - 1)], res_sem.at[1, 0])
+        wait_bytes(plane_res.at[pl.ds(0, plane - 1)], res_sem.at[2, 0])
+        sum_copy().wait_send()
+
+    @pl.when(c == 0)
+    def _():
+        for it in range(ITERS):
+            map_copy(it).wait_send()
+        twin_res_copy().wait_send()
+        sum_copy().wait_recv()
+
+    sums_ref[...] = sum_row[...]
     for it in range(ITERS):
         wait_bytes(sent.at[it, pl.ds(0, 3)], send_sem.at[it])
-        wait_bytes(line_maps.at[it, pl.ds(0, members - 1)], line_sem.at[it, 0])
-        wait_bytes(x_maps.at[it, pl.ds(0, nx - 1)], x_sem.at[it, 0])
-    wait_bytes(line_res.at[pl.ds(0, members - 1)], res_sem.at[0])
-    wait_bytes(plane_res.at[pl.ds(0, plane - 1)], res_sem.at[2])
-
-
-def write_out(count, hist, plane_res, out_hbm, res_ref, out_sem):
+
+
+def write_out(count, hist, sums_ref, out_hbm, res_ref, out_sem):
     steps = hist.shape[0] - 1
     copies = [
         pltpu.make_async_copy(
@@ -438,8 +483,7 @@
     ]
     for copy in copies:
         copy.start()
-    sums = functools.reduce(jnp.add, [plane_res[k] for k in range(plane_res.shape[0])])
-    norms = jnp.sqrt(jnp.sum(sums, 1, keepdims=True) / count)
+    norms = jnp.sqrt(jnp.sum(sums_ref[...], 1, keepdims=True) / count)
     for it in range(ITERS):
         res_ref[it] = norms[it, 0]
     for copy in copies:
@@ -456,16 +500,15 @@
     rows, width = guess.shape
     vocab, full = input_table.shape[0], recur_weight.shape[0]
     nx, nz, nc, ny = (lax.axis_size(a) for a in (*TM, "hid"))
-    steps, members, plane, tiles = rows // SEGS, nz * nc, nx * ny, width // LANES
-    group = steps // PAIRS
+    steps, plane, tiles = rows // SEGS, nx * ny, width // LANES
     anywhere = pl.BlockSpec(memory_space=pl.ANY)
     vmem = pl.BlockSpec(memory_space=pltpu.VMEM)
     sem = pltpu.SemaphoreType.DMA
-    hist, plane_res = pl.pallas_call(
+    hist, sums = pl.pallas_call(
         functools.partial(kernel, (nx, nz, nc, ny, rows, width, vocab)),
         out_shape=(
             pltpu.VMEM((steps + 1, SEGS, width), F32),
-            pltpu.VMEM((plane, ITERS, LANES), F32),
+            pltpu.VMEM((ITERS, LANES), F32),
         ),
         in_specs=[pl.BlockSpec(memory_space=pltpu.HBM)] * 7,
         out_specs=(vmem, vmem),
@@ -486,9 +529,17 @@
             pltpu.VMEM((3, SEGS, width), F32),
             pltpu.VMEM((2, SEGS, width), F32),
             pltpu.VMEM((SEGS, width), F32),
-            pltpu.VMEM((ITERS, members, 2 * tiles, LANES), F32),
+            pltpu.VMEM((ITERS, 2 * tiles, LANES), F32),
+            pltpu.VMEM((ITERS, 2 * tiles, LANES), F32),
+            pltpu.VMEM((ITERS, nz, 2 * tiles, LANES), F32),
             pltpu.VMEM((ITERS, nx, 2 * tiles, LANES), F32),
-            pltpu.VMEM((members, ITERS, LANES), F32),
+            pltpu.VMEM((ITERS, tiles, LANES), F32),
+            pltpu.VMEM((tiles, LANES), F32),
+            pltpu.VMEM((ITERS, LANES), F32),
+            pltpu.VMEM((ITERS, LANES), F32),
+            pltpu.VMEM((nz, ITERS, LANES), F32),
+            pltpu.VMEM((plane, ITERS, LANES), F32),
+            pltpu.VMEM((ITERS, LANES), F32),
             sem((SEGS + 4,)),
             sem((2,)),
             sem((2,)),
@@ -497,7 +548,9 @@
             sem((ITERS, 2, PAIRS)),
             sem((ITERS, 2)),
             sem((ITERS, 2)),
-            sem((4,)),
+            sem((ITERS, 2)),
+            sem((ITERS, 2)),
+            sem((4, 2)),
         ],
         compiler_params=pltpu.CompilerParams(
             collective_id=0, has_side_effects=True, vmem_limit_bytes=40 * 1024 * 1024
@@ -517,7 +570,7 @@
         )
     )
     return pl.pallas_call(
-        functools.partial(write_out, nx * members * rows * ny * width),
+        functools.partial(write_out, nx * nz * nc * rows * ny * width),
         out_shape=(
             jax.ShapeDtypeStruct((rows, width), F32),
             jax.ShapeDtypeStruct((ITERS,), F32),
@@ -526,7 +579,7 @@
         out_specs=(anywhere, pl.BlockSpec(memory_space=pltpu.SMEM)),
         scratch_shapes=[sem((SEGS,))],
         compiler_params=pltpu.CompilerParams(vmem_limit_bytes=8 * 1024 * 1024),
-    )(hist, plane_res)
+    )(hist, sums)
 
 
 def solution(mesh):

time: 73.4 us -> 71.2 us (0.970)
  Pallas kernels: 72.6 us -> 70.5 us
    pallas_call x1, Pallas kernels: 71 us -> 68.9 us  [per_device(): pl.pallas_call(functools.partial(kernel, (nx, nz, nc, ny, rows, width, vo...]
where the time goes in v2:
time: 71.2 us; the launch traced here: 71.1 us
  Pallas kernels  70.5 us (99%)
    pallas_call x1, Pallas kernels, per_device(): pl.pallas_call(functools.partial(kernel, (nx, nz, nc, ny, rows, width, vo...  68.9 us
    pallas_call x1, Pallas kernels, per_device(): pl.pallas_call(functools.partial(write_out, nx * nz * nc * rows * ny * wi...  1.55 us

profile of v2, /device:TPU:1, one launch (start us, length us, event | category | flops | bytes accessed | tf_op | source)
XLA Modules:
  0.0 71.1 jit_solution(7342693407424482366)
XLA Ops:
  0.6 68.9 %shard_map.86 = (f32[65,8,512]{2,1,0:T(8,128)S(1)}, f32[2,128]{1,0:T(2,128)S(1)}) custom-call(s32[1,512]{1,0:T(1,128)} %bitcast.8, f32[3,256,512]{2,1,0:T(8,128)} %bitcast.7, bf16[3,2048,512]{2,1,0:T(8,128)(2,1)} %bitcast.6, f32[1,512]{1,0:T(1,128)} %bitcast.9, f32[1,512]{1,0:T(1,128)} %bitcast.10, f32[1,512]{1,0:T(1,128)} %bitcast.11, f32[512,512]{1,0:T(8,128)} %guess_hbm.1), custom_call_target="tpu_custom_call" | custom-call | tf_op jit(solution)/shard_map/pallas_call | solution.py:507
  69.6 1.5 %shard_map.87 = (f32[512,512]{1,0:T(8,128)}, f32[2]{0:T(128)}) custom-call(f32[65,8,512]{2,1,0:T(8,128)S(1)} %get-tuple-element.4.hist, f32[2,128]{1,0:T(2,128)S(1)} %get-tuple-element.5.sums_ref), custom_call_target="tpu_custom_call" | custom-call | tf_op jit(solution)/shard_map/pallas_call | solution.py:572

commit v3 on v2

--- a/solution.py
+++ b/solution.py
@@ -10,9 +10,9 @@
 
 ITERS = 2
 SEGS = 8
-PAIRS = 4
+BLOCKS = 4
 LANES = 128
-ORDERS = ((1, 0, 2, 3), (0, 1, 2, 3))
+ORDERS = ((1, 0, 2, 3), tuple(range(BLOCKS)))
 TM = ("tm_0", "tm_1", "tm_2")
 MESH = pl.DeviceIdType.MESH
 F32 = jnp.float32
@@ -66,14 +66,10 @@
     diag,
     seg,
     edge,
-    own_map,
-    twin_map,
     z_maps,
     x_maps,
     enter_row,
     here,
-    own_res,
-    twin_res,
     z_res,
     plane_res,
     sum_row,
@@ -83,7 +79,6 @@
     send_sem,
     recv_sem,
     relay_sem,
-    map_sem,
     z_sem,
     x_sem,
     enter_sem,
@@ -91,21 +86,22 @@
 ):
     nx, nz, nc, ny, rows, width, vocab = dims
     steps = rows // SEGS
-    block = rows // PAIRS
+    block = rows // BLOCKS
     group = block // SEGS
     tiles = width // LANES
     members = nz * nc
     plane = nx * ny
     x, z, c, y = (lax.axis_index(a) for a in (*TM, "hid"))
     tm = x * members + z * nc + c
+    mine = z * nc + c
     twin = {"tm_2": 1 - c}
     right, left, far = (lax.rem(y + d, ny) for d in (1, ny - 1, 2))
 
     def far_first(k, size):
         return size // 2 + k // 2 * (1 - 2 * lax.rem(k, 2))
 
-    def z_peer(k):
-        return {"tm_1": lax.rem(z + far_first(k, nz), nz)}
+    def z_peer(k, core):
+        return {"tm_1": lax.rem(z + far_first(k, nz), nz), "tm_2": core}
 
     def x_peer(k):
         return {"tm_0": lax.rem(x + far_first(k, nx), nx)}
@@ -135,7 +131,8 @@
     greet(tm_peer(before))
     greet(twin)
     each(plane, lambda k: greet(plane_peer(k)))
-    each(nz, lambda k: greet(z_peer(k)))
+    for core in range(nc):
+        each(nz, lambda k: greet(z_peer(k, core)))
 
     for s in range(SEGS):
         pltpu.make_async_copy(
@@ -155,7 +152,7 @@
         copy.start()
     table_copy = pltpu.make_async_copy(table_hbm, table, weight_sem.at[0])
     weight_copy = pltpu.make_async_copy(weight_hbm, weight, weight_sem.at[1])
-    pl.semaphore_wait(barrier, plane + nz + 1)
+    pl.semaphore_wait(barrier, plane + 2 + nc * (nz - 1))
 
     edge_copy = pltpu.make_async_remote_copy(
         src_ref=hist.at[steps],
@@ -221,7 +218,7 @@
 
             lax.fori_loop(0, 3, gate, None)
 
-        lax.fori_loop(0, PAIRS, visit, None)
+        lax.fori_loop(0, BLOCKS, visit, None)
 
     def far_products(it, p):
         relay(it, p, 0, far).wait_recv()
@@ -279,23 +276,18 @@
             device_id_type=MESH,
         )
 
-    def map_copy(it):
-        return send(own_map.at[it], twin_map.at[it], map_sem.at[it], twin)
-
-    def z_copy(it, k):
-        return send(z_maps.at[it, z], z_maps.at[it, z], z_sem.at[it], z_peer(k))
+    def to_line(slot, sems):
+        each(nz, lambda k: send(slot, slot, sems, z_peer(k, 1)).start())
+
+        @pl.when(c == 0)
+        def _():
+            send(slot, slot, sems, twin).start()
 
     def x_copy(it, k):
         return send(x_maps.at[it, x], x_maps.at[it, x], x_sem.at[it], x_peer(k))
 
     def enter_copy(it):
         return send(enter_row.at[it], enter_row.at[it], enter_sem.at[it], twin)
-
-    def twin_res_copy():
-        return send(own_res, twin_res, res_sem.at[0], twin)
-
-    def z_res_copy(k):
-        return send(z_res.at[z], z_res.at[z], res_sem.at[1], z_peer(k))
 
     def plane_copy(k):
         slot = plane_res.at[x * ny + y]
@@ -309,52 +301,42 @@
 
     def entering(it, run_a, run_b, sums):
         if sums is not None:
-            own_res[...] = jnp.concatenate([jnp.sum(e, 0, keepdims=True) for e in sums], 0)
-
-            @pl.when(c == 0)
-            def _():
-                twin_res_copy().start()
-
+            z_res[mine] = jnp.concatenate([jnp.sum(e, 0, keepdims=True) for e in sums], 0)
+            to_line(z_res.at[mine], res_sem.at[1])
         map_a, map_b = jnp.ones((1, width), F32), jnp.zeros((1, width), F32)
         for s in range(SEGS):
             seg[0, s : s + 1] = map_a
             seg[1, s : s + 1] = map_b
             map_b = run_a[s : s + 1] * map_b + run_b[s : s + 1]
             map_a = run_a[s : s + 1] * map_a
-        own_map[it] = jnp.concatenate([lanes_to_rows(map_a), lanes_to_rows(map_b)], 0)
+        z_maps[it, mine] = jnp.concatenate([lanes_to_rows(map_a), lanes_to_rows(map_b)], 0)
+        to_line(z_maps.at[it, mine], z_sem.at[it])
 
         @pl.when(c == 0)
         def _():
-            map_copy(it).start()
             enter_copy(it).wait_recv()
             here[...] = enter_row[it]
 
         @pl.when(c == 1)
         def _():
-            map_copy(it).wait_recv()
-            twin_a, twin_b = halves(twin_map[it])
-            last_a, last_b = halves(own_map[it])
-            z_maps[it, z] = jnp.concatenate([last_a * twin_a, last_a * twin_b + last_b], 0)
-            each(nz, lambda k: z_copy(it, k).start())
             if sums is not None:
-                twin_res_copy().wait_recv()
-                z_res[z] = own_res[...] + twin_res[...]
-                each(nz, lambda k: z_res_copy(k).start())
-            wait_bytes(z_maps.at[it, pl.ds(0, nz - 1)], z_sem.at[it, 1])
+                wait_bytes(z_res.at[pl.ds(0, members - 1)], res_sem.at[1, 1])
+                plane_res[x * ny + y] = functools.reduce(
+                    jnp.add, [z_res[k] for k in range(members)]
+                )
+                each(plane, lambda k: plane_copy(k).start())
+            wait_bytes(z_maps.at[it, pl.ds(0, members - 1)], z_sem.at[it, 1])
             all_a, all_b = jnp.ones((tiles, LANES), F32), jnp.zeros((tiles, LANES), F32)
             own_a, own_b = all_a, all_b
-            for k in range(nz):
+            for k in range(members):
                 step_a, step_b = halves(z_maps[it, k])
                 all_b = step_a * all_b + step_b
                 all_a = step_a * all_a
-                own_a = jnp.where(z == k + 1, all_a, own_a)
-                own_b = jnp.where(z == k + 1, all_b, own_b)
+                if k % nc == nc - 1:
+                    own_a = jnp.where(mine == k + nc, all_a, own_a)
+                    own_b = jnp.where(mine == k + nc, all_b, own_b)
             x_maps[it, x] = jnp.concatenate([all_a, all_b], 0)
             each(nx, lambda k: x_copy(it, k).start())
-            if sums is not None:
-                wait_bytes(z_res.at[pl.ds(0, nz - 1)], res_sem.at[1, 1])
-                plane_res[x * ny + y] = functools.reduce(jnp.add, [z_res[k] for k in range(nz)])
-                each(plane, lambda k: plane_copy(k).start())
             wait_bytes(x_maps.at[it, pl.ds(0, nx - 1)], x_sem.at[it, 1])
             held = lanes_to_rows(init_ref[...])
             for k in range(nx):
@@ -363,6 +345,7 @@
             held = own_a * held + own_b
             enter_row[it] = held
             enter_copy(it).start()
+            twin_a, twin_b = halves(z_maps[it, z * nc])
             here[...] = twin_a * held + twin_b
 
         return seg[0] * rows_to_lanes(here[...]) + seg[1]
@@ -420,7 +403,7 @@
                 found += zb_ref[...]
             inp[g, block_rows(p)] = found
 
-    lax.fori_loop(0, PAIRS, look_up, None)
+    lax.fori_loop(0, BLOCKS, look_up, None)
 
     weight_copy.wait()
     same = lax.broadcasted_iota(jnp.int32, (LANES, LANES), 0) == lax.broadcasted_iota(
@@ -445,7 +428,7 @@
     second_sum = sum_tiles(second_err)
     enter = entering(1, run_a, run_b, (first_sum, second_sum))
 
-    for p in range(PAIRS):
+    for p in range(BLOCKS):
         apply(p, enter)
 
     @pl.when(c == 1)
@@ -464,8 +447,8 @@
     @pl.when(c == 0)
     def _():
         for it in range(ITERS):
-            map_copy(it).wait_send()
-        twin_res_copy().wait_send()
+            wait_bytes(z_maps.at[it, pl.ds(0, nz)], z_sem.at[it, 0])
+        wait_bytes(z_res.at[pl.ds(0, nz)], res_sem.at[1, 0])
         sum_copy().wait_recv()
 
     sums_ref[...] = sum_row[...]
@@ -529,24 +512,19 @@
             pltpu.VMEM((3, SEGS, width), F32),
             pltpu.VMEM((2, SEGS, width), F32),
             pltpu.VMEM((SEGS, width), F32),
-            pltpu.VMEM((ITERS, 2 * tiles, LANES), F32),
-            pltpu.VMEM((ITERS, 2 * tiles, LANES), F32),
-            pltpu.VMEM((ITERS, nz, 2 * tiles, LANES), F32),
+            pltpu.VMEM((ITERS, nz * nc, 2 * tiles, LANES), F32),
             pltpu.VMEM((ITERS, nx, 2 * tiles, LANES), F32),
             pltpu.VMEM((ITERS, tiles, LANES), F32),
             pltpu.VMEM((tiles, LANES), F32),
-            pltpu.VMEM((ITERS, LANES), F32),
-            pltpu.VMEM((ITERS, LANES), F32),
-            pltpu.VMEM((nz, ITERS, LANES), F32),
+            pltpu.VMEM((nz * nc, ITERS, LANES), F32),
             pltpu.VMEM((plane, ITERS, LANES), F32),
             pltpu.VMEM((ITERS, LANES), F32),
             sem((SEGS + 4,)),
             sem((2,)),
             sem((2,)),
             sem((ITERS,)),
-            sem((ITERS, 2, PAIRS)),
-            sem((ITERS, 2, PAIRS)),
-            sem((ITERS, 2)),
+            sem((ITERS, 2, BLOCKS)),
+            sem((ITERS, 2, BLOCKS)),
             sem((ITERS, 2)),
             sem((ITERS, 2)),
             sem((ITERS, 2)),

time: 71.2 us -> 70.4 us (0.989)
  Pallas kernels: 70.5 us -> 69.7 us
    pallas_call x1, Pallas kernels: 68.9 us -> 68.1 us  [per_device(): pl.pallas_call(functools.partial(kernel, (nx, nz, nc, ny, rows, width, vo...]
where the time goes in v3:
time: 70.4 us; the launch traced here: 70.3 us
  Pallas kernels  69.7 us (99%)
    pallas_call x1, Pallas kernels, per_device(): pl.pallas_call(functools.partial(kernel, (nx, nz, nc, ny, rows, width, vo...  68.1 us
    pallas_call x1, Pallas kernels, per_device(): pl.pallas_call(functools.partial(write_out, nx * nz * nc * rows * ny * wi...  1.55 us

profile of v3, /device:TPU:1, one launch (start us, length us, event | category | flops | bytes accessed | tf_op | source)
XLA Modules:
  0.0 70.3 jit_solution(17432190136618203750)
XLA Ops:
  0.6 68.1 %shard_map.86 = (f32[65,8,512]{2,1,0:T(8,128)S(1)}, f32[2,128]{1,0:T(2,128)S(1)}) custom-call(s32[1,512]{1,0:T(1,128)} %bitcast.8, f32[3,256,512]{2,1,0:T(8,128)} %bitcast.7, bf16[3,2048,512]{2,1,0:T(8,128)(2,1)} %bitcast.6, f32[1,512]{1,0:T(1,128)} %bitcast.9, f32[1,512]{1,0:T(1,128)} %bitcast.10, f32[1,512]{1,0:T(1,128)} %bitcast.11, f32[512,512]{1,0:T(8,128)} %guess_hbm.1), custom_call_target="tpu_custom_call" | custom-call | tf_op jit(solution)/shard_map/pallas_call | solution.py:490
  68.8 1.5 %shard_map.87 = (f32[512,512]{1,0:T(8,128)}, f32[2]{0:T(128)}) custom-call(f32[65,8,512]{2,1,0:T(8,128)S(1)} %get-tuple-element.4.hist, f32[2,128]{1,0:T(2,128)S(1)} %get-tuple-element.5.sums_ref), custom_call_target="tpu_custom_call" | custom-call | tf_op jit(solution)/shard_map/pallas_call | solution.py:550

commit v4 on v3

--- a/solution.py
+++ b/solution.py
@@ -73,6 +73,8 @@
     z_res,
     plane_res,
     sum_row,
+    lead_maps,
+    enters,
     in_sem,
     weight_sem,
     edge_sem,
@@ -83,11 +85,14 @@
     x_sem,
     enter_sem,
     res_sem,
+    lead_sem,
 ):
     nx, nz, nc, ny, rows, width, vocab = dims
     steps = rows // SEGS
     block = rows // BLOCKS
     group = block // SEGS
+    lead = rows // 16
+    lead_steps = lead // SEGS - 1
     tiles = width // LANES
     members = nz * nc
     plane = nx * ny
@@ -165,10 +170,66 @@
     edge_copy.start()
 
     def piece(it, slot, p):
-        return sent.at[it, slot, pl.ds(p * block, block)]
+        skip = lead if it and isinstance(p, int) and p == 0 else 0
+        return sent.at[it, slot, pl.ds(p * block + skip, block - skip)]
 
     def half(it, slot, p, h):
-        return sent.at[it, slot, pl.ds(p * block + h * (block // 2), block // 2)]
+        skip = lead if it and isinstance(p, int) and p == 0 else 0
+        size = (block - skip) // 2
+        return sent.at[it, slot, pl.ds(p * block + skip + h * size, size)]
+
+    def lead_copy(part, side, slot):
+        source = (pre_a, pre_b)[part].at[pl.ds(0, lead_steps)]
+        return pltpu.make_async_remote_copy(
+            src_ref=source,
+            dst_ref=lead_maps.at[slot, part],
+            send_sem=lead_sem.at[0],
+            recv_sem=lead_sem.at[2 + 2 * side + part],
+            device_id={"hid": (right, left)[side]},
+            device_id_type=MESH,
+        )
+
+    def lead_relay(side, slot):
+        return pltpu.make_async_remote_copy(
+            src_ref=lead_maps.at[slot, side],
+            dst_ref=lead_maps.at[slot, side],
+            send_sem=lead_sem.at[0],
+            recv_sem=lead_sem.at[6 + side],
+            device_id={"hid": (right, left)[side]},
+            device_id_type=MESH,
+        )
+
+    def lead_enter(k, slot):
+        return pltpu.make_async_remote_copy(
+            src_ref=enters.at[slot],
+            dst_ref=enters.at[slot],
+            send_sem=lead_sem.at[1],
+            recv_sem=lead_sem.at[8 + k],
+            device_id={"hid": (right, left, far)[k]},
+            device_id_type=MESH,
+        )
+
+    def start_lead():
+        for side in range(2):
+            for part in range(2):
+                lead_copy(part, side, y).start()
+
+    def forward_lead():
+        for side, slot in ((0, left), (1, right)):
+            for part in range(2):
+                lead_copy(part, side, slot).wait_recv()
+            lead_relay(side, slot).start()
+
+    def fill_lead():
+        for side in range(2):
+            lead_relay(side, far).wait_recv()
+        for k, slot in enumerate((left, right, far)):
+            lead_enter(k, slot).wait_recv()
+            state = enters[slot]
+            prev = [state] + [
+                lead_maps[slot, 0, j] * state + lead_maps[slot, 1, j] for j in range(lead_steps)
+            ]
+            sent[1, slot, 0:lead] = jnp.concatenate(prev, 0).astype(BF16)
 
     def direct(it, p, side, slot):
         return pltpu.make_async_remote_copy(
@@ -203,12 +264,13 @@
         direct(it, p, 1, y).start()
 
     def near_products(it):
-        def visit(i, _):
-            p = jnp.where(i < 2, 1 - i, i) if it == 0 else i
+        def visit(p, _):
             direct(it, p, 0, left).wait_recv()
             relay(it, p, 0, left).start()
             direct(it, p, 1, right).wait_recv()
             relay(it, p, 1, right).start()
+            if it and isinstance(p, int):
+                fill_lead()
 
             def gate(g, _):
                 part = dot(sent[it, y, block_rows(p)], weight[g, weight_rows(y)])
@@ -218,7 +280,12 @@
 
             lax.fori_loop(0, 3, gate, None)
 
-        lax.fori_loop(0, BLOCKS, visit, None)
+        if it:
+            visit(0, None)
+            lax.fori_loop(1, BLOCKS, visit, None)
+            wait_bytes(lead_maps.at[pl.ds(0, 3)], lead_sem.at[0])
+        else:
+            lax.fori_loop(0, BLOCKS, lambda i, _: visit(jnp.where(i < 2, 1 - i, i), None), None)
 
     def far_products(it, p):
         relay(it, p, 0, far).wait_recv()
@@ -311,9 +378,13 @@
             map_a = run_a[s : s + 1] * map_a
         z_maps[it, mine] = jnp.concatenate([lanes_to_rows(map_a), lanes_to_rows(map_b)], 0)
         to_line(z_maps.at[it, mine], z_sem.at[it])
+        if sums is None:
+            start_lead()
 
         @pl.when(c == 0)
         def _():
+            if sums is None:
+                forward_lead()
             enter_copy(it).wait_recv()
             here[...] = enter_row[it]
 
@@ -337,6 +408,8 @@
                     own_b = jnp.where(mine == k + nc, all_b, own_b)
             x_maps[it, x] = jnp.concatenate([all_a, all_b], 0)
             each(nx, lambda k: x_copy(it, k).start())
+            if sums is None:
+                forward_lead()
             wait_bytes(x_maps.at[it, pl.ds(0, nx - 1)], x_sem.at[it, 1])
             held = lanes_to_rows(init_ref[...])
             for k in range(nx):
@@ -419,6 +492,9 @@
     run_a, run_b, first_err = sweep(0)
     enter = entering(0, run_a, run_b, None)
     hist[0] = enter
+    enters[y] = enter
+    for k in range(3):
+        lead_enter(k, y).start()
     for p in ORDERS[1]:
         apply(p, enter)
         send_block(1, p)
@@ -452,8 +528,10 @@
         sum_copy().wait_recv()
 
     sums_ref[...] = sum_row[...]
+    wait_bytes(enters.at[pl.ds(0, 3)], lead_sem.at[1])
     for it in range(ITERS):
-        wait_bytes(sent.at[it, pl.ds(0, 3)], send_sem.at[it])
+        skip = lead if it else 0
+        wait_bytes(sent.at[it, pl.ds(0, 3), pl.ds(skip, rows - skip)], send_sem.at[it])
 
 
 def write_out(count, hist, sums_ref, out_hbm, res_ref, out_sem):
@@ -519,6 +597,8 @@
             pltpu.VMEM((nz * nc, ITERS, LANES), F32),
             pltpu.VMEM((plane, ITERS, LANES), F32),
             pltpu.VMEM((ITERS, LANES), F32),
+            pltpu.VMEM((ny, 2, steps // 16 - 1, SEGS, width), F32),
+            pltpu.VMEM((ny, SEGS, width), F32),
             sem((SEGS + 4,)),
             sem((2,)),
             sem((2,)),
@@ -529,6 +609,7 @@
             sem((ITERS, 2)),
             sem((ITERS, 2)),
             sem((4, 2)),
+            sem((11,)),
         ],
         compiler_params=pltpu.CompilerParams(
             collective_id=0, has_side_effects=True, vmem_limit_bytes=40 * 1024 * 1024

time: 70.4 us -> 70.2 us (level)
  no operation moved by 1% of the time
where the time goes in v4:
time: 70.2 us; the launch traced here: 70.1 us
  Pallas kernels  69.5 us (99%)
    pallas_call x1, Pallas kernels, per_device(): pl.pallas_call(functools.partial(kernel, (nx, nz, nc, ny, rows, width, vo...  67.9 us
    pallas_call x1, Pallas kernels, per_device(): pl.pallas_call(functools.partial(write_out, nx * nz * nc * rows * ny * wi...  1.55 us

profile of v4, /device:TPU:1, one launch (start us, length us, event | category | flops | bytes accessed | tf_op | source)
XLA Modules:
  0.0 70.1 jit_solution(16069548749101801558)
XLA Ops:
  0.6 67.9 %shard_map.86 = (f32[65,8,512]{2,1,0:T(8,128)S(1)}, f32[2,128]{1,0:T(2,128)S(1)}) custom-call(s32[1,512]{1,0:T(1,128)} %bitcast.8, f32[3,256,512]{2,1,0:T(8,128)} %bitcast.7, bf16[3,2048,512]{2,1,0:T(8,128)(2,1)} %bitcast.6, f32[1,512]{1,0:T(1,128)} %bitcast.9, f32[1,512]{1,0:T(1,128)} %bitcast.10, f32[1,512]{1,0:T(1,128)} %bitcast.11, f32[512,512]{1,0:T(8,128)} %guess_hbm.1), custom_call_target="tpu_custom_call" | custom-call | tf_op jit(solution)/shard_map/pallas_call | solution.py:568
  68.6 1.5 %shard_map.87 = (f32[512,512]{1,0:T(8,128)}, f32[2]{0:T(128)}) custom-call(f32[65,8,512]{2,1,0:T(8,128)S(1)} %get-tuple-element.4.hist, f32[2,128]{1,0:T(2,128)S(1)} %get-tuple-element.5.sums_ref), custom_call_target="tpu_custom_call" | custom-call | tf_op jit(solution)/shard_map/pallas_call | solution.py:631
